TPU v7x, 512 devices: a whole 4x4x16 slice. The times are simulated.
512 devices in a mesh: sector: 32 (over y, x, core), term: 16 (over z).
Axes of the slice: x: 4, y: 4, z: 16, core: 2. Of those that a mesh axis runs over, the one named last changes fastest.
Arguments:
- blocks: bfloat16 [20480, 640], P('sector'), may hold values from -6 to 6
- left_env: bfloat16 [32, 16, 640, 1920], P('sector', 'term'), may hold values from -0.125 to 0.125
- right_env: bfloat16 [32, 16, 640, 640], P('sector', 'term'), may hold values from -0.0625 to 0.0625
- coupling: int32 [32, 3], P('sector'), may hold values 0 or 1
- widths: int32 [32], P('sector'), may hold values from 320 to 640
Outputs:
- filtered: bfloat16 [20480, 640], P('sector')
All inputs are finite; a program needn't handle non-finite values. No bound on the sum of `coupling` on one device may be relied on, other than what follows from the above.
Results may differ from a plain program's by a relative error of at most 0.005.
Values may be sent and summed in bfloat16 or wider, within the bound.
No kernel may reach another device: no remote copies, remote signals or barrier semaphores. Data moves between devices by JAX's collectives and lax.ppermute only.
A program may use at most 64 MiB of HBM per device.

v0:
```python
import jax
import jax.numpy as jnp
from jax import lax
from jax.sharding import PartitionSpec as P


def with_halo(x, axis):
    count = lax.axis_size(axis)
    up = [(i, (i + 1) % count) for i in range(count - 1)]
    down = [(j, i) for i, j in up]
    before = lax.ppermute(x, axis, up)
    after = lax.ppermute(x, axis, down)
    return jnp.concatenate([before, x, after], axis=0)


def keep_live(values, live_width, row_offset):
    row_index = row_offset + lax.broadcasted_iota(jnp.int32, values.shape, 0)
    col_index = lax.broadcasted_iota(jnp.int32, values.shape, 1)
    return jnp.where(
        (row_index < live_width) & (col_index < live_width), values, jnp.zeros_like(values)
    )


def contract(stacked, left_part, right_part):
    partial_value = jnp.einsum(
        "ik,kj->ij", left_part, stacked, preferred_element_type=jnp.float32
    ).astype(jnp.bfloat16)
    return jnp.einsum("ij,jl->il", partial_value, right_part, preferred_element_type=jnp.float32)


def shards(blocks, left_env, right_env, coupling, widths):
    side = blocks.shape[1]
    left_part = left_env[0, 0]
    right_part = right_env[0, 0]
    live_width = widths[0]
    row_scale = jnp.repeat(coupling[0].astype(jnp.bfloat16), side)
    terms = lax.axis_size("term")
    rows = side // terms
    row_offset = lax.axis_index("term") * rows

    def apply_rows(source):
        nearby = with_halo(source, "sector")
        part = contract(nearby * row_scale[:, None], left_part, right_part)
        part = part.astype(jnp.bfloat16).reshape(terms, rows, side)
        pieces = lax.all_to_all(part, "term", 0, 0, tiled=True)
        total = jnp.sum(pieces.astype(jnp.float32), axis=0)
        return keep_live(total, live_width, row_offset)

    def gather(piece):
        return lax.all_gather(piece, "term", axis=0, tiled=True)

    first_pass = gather(apply_rows(blocks).astype(jnp.bfloat16))
    own = lax.dynamic_slice_in_dim(blocks, row_offset, rows, axis=0).astype(jnp.float32)
    return gather((2.0 * apply_rows(first_pass) - own).astype(jnp.bfloat16))


def solution(mesh):
    placed = (
        P("sector", None),
        P("sector", "term", None, None),
        P("sector", "term", None, None),
        P("sector", None),
        P("sector"),
    )
    return jax.shard_map(
        shards, mesh=mesh, in_specs=placed, out_specs=P("sector", None), check_vma=False
    )
```

profile of v0, /device:TPU:22, one launch (start us, length us, event | category | flops | bytes accessed | tf_op | source)
XLA Modules:
  0.0 220.3 jit_solution(6024967086172461485)
XLA Ops:
  0.0 0.0 copy-start
  0.0 2.3 %collective-permute-start.1 = (bf16[640,640]{1,0:T(8,128)(2,1)}, bf16[640,640]{1,0:T(8,128)(2,1)S(1)}, u32[]{:S(2)}, u32[]{:S(2)}) collective-permute-start(bf16[640,640]{1,0:T(8,128)(2,1)} %param.5), channel_id=1, source_target_pairs={{16,0},{32,16},{48,32},{64,48},{80,64},{96,80},{112,96},{128,112},... | collective-permute-start | bytes 2457608 | tf_op jit(solution)/shard_map/ppermute | solution.py:12
  2.3 2.2 collective-permute-start
  4.5 0.7 convert_bitcast_fusion
  5.1 0.1 broadcast_in_dim.3
  5.2 7.2 %collective-permute-done.1 = bf16[640,640]{1,0:T(8,128)(2,1)S(1)} collective-permute-done((bf16[640,640]{1,0:T(8,128)(2,1)}, bf16[640,640]{1,0:T(8,128)(2,1)S(1)}, u32[]{:S(2)}, u32[]{:S(2)}) %collective-permute-start.1) | collective-permute-done | bytes 819232 | tf_op jit(solution)/shard_map/ppermute | solution.py:12
  12.5 3.8 %collective-permute-done = bf16[640,640]{1,0:T(8,128)(2,1)} collective-permute-done((bf16[640,640]{1,0:T(8,128)(2,1)}, bf16[640,640]{1,0:T(8,128)(2,1)}, u32[]{:S(2)}, u32[]{:S(2)}) %collective-permute-start) | collective-permute-done | bytes 819232 | tf_op jit(solution)/shard_map/ppermute | solution.py:11
  16.3 0.0 copy-done
  16.3 6.7 %convolution_convert_fusion.1 = bf16[640,640]{1,0:T(8,128)(2,1)} fusion(bf16[1,1,640,1920]{3,2,1,0:T(8,128)(2,1)S(1)} %copy-done, bf16[640,640]{1,0:T(8,128)(2,1)S(1)} %collective-permute-done.1, bf16[640,640]{1,0:T(8,128)(2,1)} %param.5, bf16[640,640]{1,0:T(8,128)(2,1)} %collective-permute-done, bf16[1920]{0:T(1024)(128)(2,1)S(1)} %mul.26, ...), kind=kOutput, calls=%fused_computation.19 | convolution fusion | flops 2107801600 | bytes 6557440 | tf_op jit(solution)/shard_map/ij,jl->il/dot_general | solution.py:28
  23.0 15.2 %all-to-all-start = ((bf16[16,40,640]{2,1,0:T(8,128)(2,1)}), bf16[16,40,640]{2,1,0:T(8,128)(2,1)S(1)}, u32[]{:S(2)}, u32[]{:S(2)}) async-start(bf16[16,40,640]{2,1,0:T(8,128)(2,1)} %bitcast.25), calls=%async_computation | async-start | bytes 1638400 | tf_op jit(solution)/shard_map/all_to_all | solution.py:45
  38.9 40.2 %all-to-all-done = bf16[16,40,640]{2,1,0:T(8,128)(2,1)S(1)} async-done(((bf16[16,40,640]{2,1,0:T(8,128)(2,1)}), bf16[16,40,640]{2,1,0:T(8,128)(2,1)S(1)}, u32[]{:S(2)}, u32[]{:S(2)}) %all-to-all-start) | async-done | bytes 819232 | tf_op jit(solution)/shard_map/all_to_all | solution.py:45
  79.1 0.1 convert_reduce_fusion.1
  79.2 0.1 fusion.26
  79.3 36.7 %all_gather.6 = bf16[640,640]{1,0:T(8,128)(2,1)S(1)} all-gather(bf16[40,640]{1,0:T(8,128)(2,1)S(1)} %fusion.26), channel_id=1, replica_groups=mesh['sector'=32,'term'=16] {'term'}, dimensions={0}, use_global_device_ids=true | all-gather | bytes 870400 | tf_op jit(solution)/shard_map/all_gather | solution.py:50
  116.0 1.9 collective-permute-start.3
  117.9 2.4 %collective-permute-start.2 = (bf16[640,640]{1,0:T(8,128)(2,1)S(1)}, bf16[640,640]{1,0:T(8,128)(2,1)}, u32[]{:S(2)}, u32[]{:S(2)}) collective-permute-start(bf16[640,640]{1,0:T(8,128)(2,1)S(1)} %all_gather.6), channel_id=1, source_target_pairs={{0,16},{16,32},{32,48},{48,64},{64,80},{80,96},{96,112},{112,128},... | collective-permute-start | bytes 2457608 | tf_op jit(solution)/shard_map/ppermute | solution.py:11
  120.3 7.4 %collective-permute-done.3 = bf16[640,640]{1,0:T(8,128)(2,1)S(1)} collective-permute-done((bf16[640,640]{1,0:T(8,128)(2,1)S(1)}, bf16[640,640]{1,0:T(8,128)(2,1)S(1)}, u32[]{:S(2)}, u32[]{:S(2)}) %collective-permute-start.3) | collective-permute-done | bytes 819232 | tf_op jit(solution)/shard_map/ppermute | solution.py:12
  127.7 0.0 copy-start.1
  127.7 0.9 copy-done.1
  128.6 3.0 %collective-permute-done.2 = bf16[640,640]{1,0:T(8,128)(2,1)} collective-permute-done((bf16[640,640]{1,0:T(8,128)(2,1)S(1)}, bf16[640,640]{1,0:T(8,128)(2,1)}, u32[]{:S(2)}, u32[]{:S(2)}) %collective-permute-start.2) | collective-permute-done | bytes 819232 | tf_op jit(solution)/shard_map/ppermute | solution.py:11
  131.7 6.7 %convolution_convert_fusion = bf16[640,640]{1,0:T(8,128)(2,1)} fusion(bf16[1,1,640,1920]{3,2,1,0:T(8,128)(2,1)S(1)} %copy-done, bf16[640,640]{1,0:T(8,128)(2,1)} %copy-done.1, bf16[640,640]{1,0:T(8,128)(2,1)S(1)} %all_gather.6, bf16[640,640]{1,0:T(8,128)(2,1)} %collective-permute-done.2, bf16[1920]{0:T(1024)(128)(2,1)S(1)} %mul.26, ...), kind=kOutput, calls=%fused_computation.18 | convolution fusion | flops 2107801600 | bytes 6557440 | tf_op jit(solution)/shard_map/ij,jl->il/dot_general | solution.py:28
  138.4 5.2 %all-to-all-start.1 = ((bf16[16,40,640]{2,1,0:T(8,128)(2,1)}), bf16[16,40,640]{2,1,0:T(8,128)(2,1)S(1)}, u32[]{:S(2)}, u32[]{:S(2)}) async-start(bf16[16,40,640]{2,1,0:T(8,128)(2,1)} %bitcast.26), calls=%async_computation.1 | async-start | bytes 1638400 | tf_op jit(solution)/shard_map/all_to_all | solution.py:45
  143.6 37.5 %all-to-all-done.1 = bf16[16,40,640]{2,1,0:T(8,128)(2,1)S(1)} async-done(((bf16[16,40,640]{2,1,0:T(8,128)(2,1)}), bf16[16,40,640]{2,1,0:T(8,128)(2,1)S(1)}, u32[]{:S(2)}, u32[]{:S(2)}) %all-to-all-start.1) | async-done | bytes 819232 | tf_op jit(solution)/shard_map/all_to_all | solution.py:45
  181.1 0.1 convert_reduce_fusion
  181.2 0.9 fusion.29
  182.2 37.2 %all_gather.7 = bf16[640,640]{1,0:T(8,128)(2,1)S(1)} all-gather(bf16[40,640]{1,0:T(8,128)(2,1)S(1)} %fusion.29), channel_id=1, replica_groups=mesh['sector'=32,'term'=16] {'term'}, dimensions={0}, use_global_device_ids=true | all-gather | bytes 870400 | tf_op jit(solution)/shard_map/all_gather | solution.py:50
  219.4 0.9 copy.8
  (3 shorter events, 0.0 us)
Async XLA Ops:
  0.0 16.3 %copy-start = (bf16[1,1,640,1920]{3,2,1,0:T(8,128)(2,1)S(1)}, bf16[1,1,640,1920]{3,2,1,0:T(8,128)(2,1)}, u32[]{:S(2)}) copy-start(bf16[1,1,640,1920]{3,2,1,0:T(8,128)(2,1)} %param.6) | copy-start | bytes 7372804
  0.0 12.5 %collective-permute-start.1 = (bf16[640,640]{1,0:T(8,128)(2,1)}, bf16[640,640]{1,0:T(8,128)(2,1)S(1)}, u32[]{:S(2)}, u32[]{:S(2)}) collective-permute-start(bf16[640,640]{1,0:T(8,128)(2,1)} %param.5), channel_id=1, source_target_pairs={{16,0},{32,16},{48,32},{64,48},{80,64},{96,80},{112,96},{128,112},... | collective-permute-start | bytes 2457608 | tf_op jit(solution)/shard_map/ppermute | solution.py:12
  2.3 14.0 %collective-permute-start = (bf16[640,640]{1,0:T(8,128)(2,1)}, bf16[640,640]{1,0:T(8,128)(2,1)}, u32[]{:S(2)}, u32[]{:S(2)}) collective-permute-start(bf16[640,640]{1,0:T(8,128)(2,1)} %param.5), channel_id=1, source_target_pairs={{0,16},{16,32},{32,48},{48,64},{64,80},{80,96},{96,112},{112,128},... | collective-permute-start | bytes 2457608 | tf_op jit(solution)/shard_map/ppermute | solution.py:11
  23.0 56.0 %all-to-all-start = ((bf16[16,40,640]{2,1,0:T(8,128)(2,1)}), bf16[16,40,640]{2,1,0:T(8,128)(2,1)S(1)}, u32[]{:S(2)}, u32[]{:S(2)}) async-start(bf16[16,40,640]{2,1,0:T(8,128)(2,1)} %bitcast.25), calls=%async_computation | async-start | bytes 1638400 | tf_op jit(solution)/shard_map/all_to_all | solution.py:45
  116.0 11.8 %collective-permute-start.3 = (bf16[640,640]{1,0:T(8,128)(2,1)S(1)}, bf16[640,640]{1,0:T(8,128)(2,1)S(1)}, u32[]{:S(2)}, u32[]{:S(2)}) collective-permute-start(bf16[640,640]{1,0:T(8,128)(2,1)S(1)} %all_gather.6), channel_id=1, source_target_pairs={{16,0},{32,16},{48,32},{64,48},{80,64},{96,80},{112,96},{128,112},... | collective-permute-start | bytes 2457608 | tf_op jit(solution)/shard_map/ppermute | solution.py:12
  117.9 13.8 %collective-permute-start.2 = (bf16[640,640]{1,0:T(8,128)(2,1)S(1)}, bf16[640,640]{1,0:T(8,128)(2,1)}, u32[]{:S(2)}, u32[]{:S(2)}) collective-permute-start(bf16[640,640]{1,0:T(8,128)(2,1)S(1)} %all_gather.6), channel_id=1, source_target_pairs={{0,16},{16,32},{32,48},{48,64},{64,80},{80,96},{96,112},{112,128},... | collective-permute-start | bytes 2457608 | tf_op jit(solution)/shard_map/ppermute | solution.py:11
  127.7 0.9 copy-start.1
  138.4 42.7 %all-to-all-start.1 = ((bf16[16,40,640]{2,1,0:T(8,128)(2,1)}), bf16[16,40,640]{2,1,0:T(8,128)(2,1)S(1)}, u32[]{:S(2)}, u32[]{:S(2)}) async-start(bf16[16,40,640]{2,1,0:T(8,128)(2,1)} %bitcast.26), calls=%async_computation.1 | async-start | bytes 1638400 | tf_op jit(solution)/shard_map/all_to_all | solution.py:45
where the time goes:
time: 221 us; the launch traced here: 220 us
  waiting for transfers between devices  99.2 us (45%)
  blocking collectives  74 us (33%)
  starting transfers between devices  29.1 us (13%)
  matrix products  13.5 us (6%)
    all_to_all x2, waiting for transfers between devices, apply_rows(): pieces = lax.all_to_all(part, 'term', 0, 0, tiled=True)  77.7 us
    all_gather x2, blocking collectives, gather(): return lax.all_gather(piece, 'term', axis=0, tiled=True)  74 us
    all_to_all x2, starting transfers between devices, apply_rows(): pieces = lax.all_to_all(part, 'term', 0, 0, tiled=True)  20.4 us
    ppermute x2, waiting for transfers between devices, with_halo(): after = lax.ppermute(x, axis, down)  14.7 us
    dot_general x2, matrix products, contract(): jnp.einsum('ij,jl->il', partial_value, right_part, preferred_element_type...  13.5 us
    ppermute x2, waiting for transfers between devices, with_halo(): before = lax.ppermute(x, axis, up)  6.86 us
    ppermute x2, starting transfers between devices, with_halo(): before = lax.ppermute(x, axis, up)  4.56 us
  transfers between devices with their start and end apart: 6, of which 6 were waited for; matrix products, arithmetic and copies ran while one was open for 0% of the time, Pallas kernels for 0%

commit v1 on v0

--- a/solution.py
+++ b/solution.py
@@ -2,6 +2,11 @@
 import jax.numpy as jnp
 from jax import lax
 from jax.sharding import PartitionSpec as P
+
+
+def tiled_gather(x, axis, dim):
+    copies = jnp.concatenate([x] * lax.axis_size(axis), axis=dim)
+    return lax.all_to_all(copies, axis, dim, dim, tiled=True)
 
 
 def with_halo(x, axis):
@@ -47,7 +52,7 @@
         return keep_live(total, live_width, row_offset)
 
     def gather(piece):
-        return lax.all_gather(piece, "term", axis=0, tiled=True)
+        return tiled_gather(piece, "term", 0)
 
     first_pass = gather(apply_rows(blocks).astype(jnp.bfloat16))
     own = lax.dynamic_slice_in_dim(blocks, row_offset, rows, axis=0).astype(jnp.float32)

time: 221 us -> 253 us (1.14)
  blocking collectives: 74 us -> 102 us
  waiting for transfers between devices: 99.2 us -> 103 us
    all_to_all x0 -> x2, blocking collectives: none -> 102 us  [tiled_gather(): return lax.all_to_all(copies, axis, dim, dim, tiled=True)]
    all_gather x2 -> x0, blocking collectives: 74 us -> none  [gather(): return lax.all_gather(piece, 'term', axis=0, tiled=True)]
    all_to_all x2, waiting for transfers between devices: 77.7 us -> 81.4 us  [apply_rows(): pieces = lax.all_to_all(part, 'term', 0, 0, tiled=True)]
where the time goes in v1:
time: 253 us
  waiting for transfers between devices  103 us (41%)
  blocking collectives  102 us (40%)
  starting transfers between devices  29.5 us (12%)
  matrix products  13.5 us (5%)
    all_to_all x2, blocking collectives, tiled_gather(): return lax.all_to_all(copies, axis, dim, dim, tiled=True)  102 us
    all_to_all x2, waiting for transfers between devices, apply_rows(): pieces = lax.all_to_all(part, 'term', 0, 0, tiled=True)  81.4 us
    all_to_all x2, starting transfers between devices, apply_rows(): pieces = lax.all_to_all(part, 'term', 0, 0, tiled=True)  20.7 us
    ppermute x2, waiting for transfers between devices, with_halo(): after = lax.ppermute(x, axis, down)  14.7 us
    dot_general x2, matrix products, contract(): jnp.einsum('ij,jl->il', partial_value, right_part, preferred_element_type...  13.5 us
    ppermute x2, waiting for transfers between devices, with_halo(): before = lax.ppermute(x, axis, up)  6.86 us
  transfers between devices with their start and end apart: 6, of which 6 were waited for; matrix products, arithmetic and copies ran while one was open for 0% of the time, Pallas kernels for 0%

profile of v1, /device:TPU:22, one launch (start us, length us, event | category | flops | bytes accessed | tf_op | source)
XLA Modules:
  0.0 252.6 jit_solution(10730216365307867829)
XLA Ops:
  0.0 0.0 copy-start
  0.0 2.3 collective-permute-start.1
  2.3 2.2 collective-permute-start
  4.5 0.7 convert_bitcast_fusion
  5.1 0.1 broadcast_in_dim.3
  5.2 7.2 %collective-permute-done.1 = bf16[640,640]{1,0:T(8,128)(2,1)S(1)} collective-permute-done((bf16[640,640]{1,0:T(8,128)(2,1)}, bf16[640,640]{1,0:T(8,128)(2,1)S(1)}, u32[]{:S(2)}, u32[]{:S(2)}) %collective-permute-start.1) | collective-permute-done | bytes 819232 | tf_op jit(solution)/shard_map/ppermute | solution.py:17
  12.5 3.8 %collective-permute-done = bf16[640,640]{1,0:T(8,128)(2,1)} collective-permute-done((bf16[640,640]{1,0:T(8,128)(2,1)}, bf16[640,640]{1,0:T(8,128)(2,1)}, u32[]{:S(2)}, u32[]{:S(2)}) %collective-permute-start) | collective-permute-done | bytes 819232 | tf_op jit(solution)/shard_map/ppermute | solution.py:16
  16.3 0.0 copy-done
  16.3 6.7 %convolution_convert_fusion.1 = bf16[640,640]{1,0:T(8,128)(2,1)} fusion(bf16[1,1,640,1920]{3,2,1,0:T(8,128)(2,1)S(1)} %copy-done, bf16[640,640]{1,0:T(8,128)(2,1)S(1)} %collective-permute-done.1, bf16[640,640]{1,0:T(8,128)(2,1)} %param.5, bf16[640,640]{1,0:T(8,128)(2,1)} %collective-permute-done, bf16[1920]{0:T(1024)(128)(2,1)S(1)} %mul.26, ...), kind=kOutput, calls=%fused_computation.19 | convolution fusion | flops 2107801600 | bytes 6557440 | tf_op jit(solution)/shard_map/ij,jl->il/dot_general | solution.py:33
  23.0 15.2 %all-to-all-start = ((bf16[16,40,640]{2,1,0:T(8,128)(2,1)}), bf16[16,40,640]{2,1,0:T(8,128)(2,1)S(1)}, u32[]{:S(2)}, u32[]{:S(2)}) async-start(bf16[16,40,640]{2,1,0:T(8,128)(2,1)} %bitcast.32), calls=%async_computation | async-start | bytes 1638400 | tf_op jit(solution)/shard_map/all_to_all | solution.py:50
  38.9 40.2 %all-to-all-done = bf16[16,40,640]{2,1,0:T(8,128)(2,1)S(1)} async-done(((bf16[16,40,640]{2,1,0:T(8,128)(2,1)}), bf16[16,40,640]{2,1,0:T(8,128)(2,1)S(1)}, u32[]{:S(2)}, u32[]{:S(2)}) %all-to-all-start) | async-done | bytes 819232 | tf_op jit(solution)/shard_map/all_to_all | solution.py:50
  79.1 0.1 convert_reduce_fusion.1
  79.2 0.1 constant_dynamic-update-slice_fusion.15
  79.5 50.9 %all_to_all.34 = bf16[16,40,640]{2,1,0:T(8,128)(2,1)S(1)} all-to-all(bf16[16,40,640]{2,1,0:T(8,128)(2,1)S(1)} %bitcast.30), channel_id=1, replica_groups=mesh['sector'=32,'term'=16] {'term'}, dimensions={0} | all-to-all | bytes 1638400 | tf_op jit(solution)/shard_map/all_to_all | solution.py:9
  130.4 1.9 collective-permute-start.3
  132.3 2.4 collective-permute-start.2
  134.7 7.4 %collective-permute-done.3 = bf16[640,640]{1,0:T(8,128)(2,1)S(1)} collective-permute-done((bf16[640,640]{1,0:T(8,128)(2,1)S(1)}, bf16[640,640]{1,0:T(8,128)(2,1)S(1)}, u32[]{:S(2)}, u32[]{:S(2)}) %collective-permute-start.3) | collective-permute-done | bytes 819232 | tf_op jit(solution)/shard_map/ppermute | solution.py:17
  142.1 0.0 copy-start.1
  142.1 0.9 copy-done.1
  143.0 3.0 %collective-permute-done.2 = bf16[640,640]{1,0:T(8,128)(2,1)} collective-permute-done((bf16[640,640]{1,0:T(8,128)(2,1)S(1)}, bf16[640,640]{1,0:T(8,128)(2,1)}, u32[]{:S(2)}, u32[]{:S(2)}) %collective-permute-start.2) | collective-permute-done | bytes 819232 | tf_op jit(solution)/shard_map/ppermute | solution.py:16
  146.1 6.8 %convolution_convert_fusion = bf16[640,640]{1,0:T(8,128)(2,1)} fusion(bf16[1,1,640,1920]{3,2,1,0:T(8,128)(2,1)S(1)} %copy-done, bf16[640,640]{1,0:T(8,128)(2,1)} %copy-done.1, bf16[640,640]{1,0:T(8,128)(2,1)S(1)} %bitcast.35, bf16[640,640]{1,0:T(8,128)(2,1)} %collective-permute-done.2, bf16[1920]{0:T(1024)(128)(2,1)S(1)} %mul.26, ...), kind=kOutput, calls=%fused_computation.18 | convolution fusion | flops 2107801600 | bytes 6557440 | tf_op jit(solution)/shard_map/ij,jl->il/dot_general | solution.py:33
  152.8 5.5 %all-to-all-start.2 = ((bf16[16,40,640]{2,1,0:T(8,128)(2,1)}), bf16[16,40,640]{2,1,0:T(8,128)(2,1)S(1)}, u32[]{:S(2)}, u32[]{:S(2)}) async-start(bf16[16,40,640]{2,1,0:T(8,128)(2,1)} %bitcast.36), calls=%async_computation.2 | async-start | bytes 1638400 | tf_op jit(solution)/shard_map/all_to_all | solution.py:50
  158.4 41.2 %all-to-all-done.2 = bf16[16,40,640]{2,1,0:T(8,128)(2,1)S(1)} async-done(((bf16[16,40,640]{2,1,0:T(8,128)(2,1)}), bf16[16,40,640]{2,1,0:T(8,128)(2,1)S(1)}, u32[]{:S(2)}, u32[]{:S(2)}) %all-to-all-start.2) | async-done | bytes 819232 | tf_op jit(solution)/shard_map/all_to_all | solution.py:50
  199.6 0.1 convert_reduce_fusion
  199.7 0.9 constant_dynamic-update-slice_fusion.31
  200.9 50.8 %all_to_all.35 = bf16[16,40,640]{2,1,0:T(8,128)(2,1)S(1)} all-to-all(bf16[16,40,640]{2,1,0:T(8,128)(2,1)S(1)} %bitcast.31), channel_id=1, replica_groups=mesh['sector'=32,'term'=16] {'term'}, dimensions={0} | all-to-all | bytes 1638400 | tf_op jit(solution)/shard_map/all_to_all | solution.py:9
  251.7 0.9 copy.38
  (33 shorter events, 0.4 us)
Async XLA Ops:
  0.0 16.3 %copy-start = (bf16[1,1,640,1920]{3,2,1,0:T(8,128)(2,1)S(1)}, bf16[1,1,640,1920]{3,2,1,0:T(8,128)(2,1)}, u32[]{:S(2)}) copy-start(bf16[1,1,640,1920]{3,2,1,0:T(8,128)(2,1)} %param.6) | copy-start | bytes 7372804
  0.0 12.5 %collective-permute-start.1 = (bf16[640,640]{1,0:T(8,128)(2,1)}, bf16[640,640]{1,0:T(8,128)(2,1)S(1)}, u32[]{:S(2)}, u32[]{:S(2)}) collective-permute-start(bf16[640,640]{1,0:T(8,128)(2,1)} %param.5), channel_id=1, source_target_pairs={{16,0},{32,16},{48,32},{64,48},{80,64},{96,80},{112,96},{128,112},... | collective-permute-start | bytes 2457608 | tf_op jit(solution)/shard_map/ppermute | solution.py:17
  2.3 14.0 %collective-permute-start = (bf16[640,640]{1,0:T(8,128)(2,1)}, bf16[640,640]{1,0:T(8,128)(2,1)}, u32[]{:S(2)}, u32[]{:S(2)}) collective-permute-start(bf16[640,640]{1,0:T(8,128)(2,1)} %param.5), channel_id=1, source_target_pairs={{0,16},{16,32},{32,48},{48,64},{64,80},{80,96},{96,112},{112,128},... | collective-permute-start | bytes 2457608 | tf_op jit(solution)/shard_map/ppermute | solution.py:16
  23.0 56.0 %all-to-all-start = ((bf16[16,40,640]{2,1,0:T(8,128)(2,1)}), bf16[16,40,640]{2,1,0:T(8,128)(2,1)S(1)}, u32[]{:S(2)}, u32[]{:S(2)}) async-start(bf16[16,40,640]{2,1,0:T(8,128)(2,1)} %bitcast.32), calls=%async_computation | async-start | bytes 1638400 | tf_op jit(solution)/shard_map/all_to_all | solution.py:50
  130.4 11.8 %collective-permute-start.3 = (bf16[640,640]{1,0:T(8,128)(2,1)S(1)}, bf16[640,640]{1,0:T(8,128)(2,1)S(1)}, u32[]{:S(2)}, u32[]{:S(2)}) collective-permute-start(bf16[640,640]{1,0:T(8,128)(2,1)S(1)} %bitcast.33), channel_id=1, source_target_pairs={{16,0},{32,16},{48,32},{64,48},{80,64},{96,80},{112,96},{128,112},... | collective-permute-start | bytes 2457608 | tf_op jit(solution)/shard_map/ppermute | solution.py:17
  132.3 13.8 %collective-permute-start.2 = (bf16[640,640]{1,0:T(8,128)(2,1)S(1)}, bf16[640,640]{1,0:T(8,128)(2,1)}, u32[]{:S(2)}, u32[]{:S(2)}) collective-permute-start(bf16[640,640]{1,0:T(8,128)(2,1)S(1)} %bitcast.34), channel_id=1, source_target_pairs={{0,16},{16,32},{32,48},{48,64},{64,80},{80,96},{96,112},{112,128},... | collective-permute-start | bytes 2457608 | tf_op jit(solution)/shard_map/ppermute | solution.py:16
  142.1 0.9 copy-start.1
  152.8 46.8 %all-to-all-start.2 = ((bf16[16,40,640]{2,1,0:T(8,128)(2,1)}), bf16[16,40,640]{2,1,0:T(8,128)(2,1)S(1)}, u32[]{:S(2)}, u32[]{:S(2)}) async-start(bf16[16,40,640]{2,1,0:T(8,128)(2,1)} %bitcast.36), calls=%async_computation.2 | async-start | bytes 1638400 | tf_op jit(solution)/shard_map/all_to_all | solution.py:50
